TPU v7x, 16 devices: a 4x2x1 block of a 4x4x8 slice. The times are simulated.
16 devices in a mesh: rep: 2 (over y, z), dp: 8 (over x, core).
Axes of the slice: x: 4, y: 2, z: 1, core: 2. Of those that a mesh axis runs over, the one named last changes fastest.
The devices are a block of a 4x4x8 slice.
Arguments:
- x: bfloat16 [16, 2048, 1024], P(('rep', 'dp')), parts along dimension 0
- dy: bfloat16 [16, 2048, 1024], P(('rep', 'dp')), parts along dimension 0
- w_gate: bfloat16 [2, 1024, 3200], P(None, 'dp')
- w_up: bfloat16 [2, 1024, 3200], P(None, 'dp')
- w_down: bfloat16 [2, 3200, 1024], P(None, 'dp')
- m_w_gate: float32 [2, 1024, 3200], P(None, 'dp')
- m_w_up: float32 [2, 1024, 3200], P(None, 'dp')
- m_w_down: float32 [2, 3200, 1024], P(None, 'dp')
- v_w_gate: float32 [2, 1024, 3200], P(None, 'dp')
- v_w_up: float32 [2, 1024, 3200], P(None, 'dp')
- v_w_down: float32 [2, 3200, 1024], P(None, 'dp')
Outputs:
- output 1: bfloat16 [4, 1024, 3200], P('rep', 'dp'), parts along dimension 0
- output 2: bfloat16 [4, 1024, 3200], P('rep', 'dp'), parts along dimension 0
- output 3: bfloat16 [4, 3200, 1024], P('rep', 'dp'), parts along dimension 0
- output 4: float32 [4, 1024, 3200], P('rep', 'dp'), parts along dimension 0
- output 5: float32 [4, 1024, 3200], P('rep', 'dp'), parts along dimension 0
- output 6: float32 [4, 3200, 1024], P('rep', 'dp'), parts along dimension 0
- output 7: float32 [4, 1024, 3200], P('rep', 'dp'), parts along dimension 0
- output 8: float32 [4, 1024, 3200], P('rep', 'dp'), parts along dimension 0
- output 9: float32 [4, 3200, 1024], P('rep', 'dp'), parts along dimension 0
There are 2 independent parts. A program takes and returns all parts, laid end to end along the dimension named above; an argument that names none is the same for every part.
All inputs are finite; a program needn't handle non-finite values.
Results may differ from a plain program's by a relative error of at most 0.0237.
Values are sent between devices in bfloat16 or wider.
A program may use at most 768 MiB of HBM per device.

v0:
```python
import jax
import jax.numpy as jnp
from jax import lax
from jax.sharding import PartitionSpec as P

NAMES = ("w_gate", "w_up", "w_down")


def matmul(a, w):
    return jnp.dot(a, w, preferred_element_type=jnp.float32).astype(jnp.bfloat16)


def normed(h):
    wide = h.astype(jnp.float32)
    scale = lax.rsqrt(jnp.mean(wide**2, -1, keepdims=True) + 1e-6)
    return (wide * scale).astype(jnp.bfloat16)


def layer(h, w):
    a = normed(h)
    gate = jnp.dot(a, w["w_gate"], preferred_element_type=jnp.float32)
    up = jnp.dot(a, w["w_up"], preferred_element_type=jnp.float32)
    return h + matmul((jax.nn.silu(gate) * up).astype(jnp.bfloat16), w["w_down"])


def adamw(w, m, v, g):
    m = 0.9 * m + 0.1 * g
    v = 0.95 * v + 0.05 * g * g
    step = m * lax.rsqrt(v + 1e-8) + 0.1 * w
    return (w - 0.02 * step).astype(jnp.bfloat16), m, v


def solution(mesh):
    def fetched(weights, number):
        return {name: lax.all_gather(w[number], "dp", axis=0, tiled=True) for name, w in zip(NAMES, weights, strict=True)}

    def step(x, dy, *arrays):
        weights, m, v = (arrays[i : i + 3] for i in (0, 3, 6))
        layers = weights[0].shape[0]
        h, kept = x[0], []
        for number in range(layers):
            kept.append(h)
            h = layer(h, fetched(weights, number))
        by_h, mine = dy[0], [None] * layers
        for number in reversed(range(layers)):
            _, back = jax.vjp(lambda w, h: layer(h, w), fetched(weights, number), kept[number])
            by_w, by_h = back(by_h)
            mine[number] = [lax.psum_scatter(by_w[name], "dp", scatter_dimension=0, tiled=True) for name in NAMES]
        gradients = [jnp.stack([mine[number][i] for number in range(layers)]).astype(jnp.float32) for i in range(3)]
        new = [adamw(w.astype(jnp.float32), m, v, g) for w, m, v, g in zip(weights, m, v, gradients, strict=True)]
        return tuple(one[which] for which in range(3) for one in new)

    states, cut = P(("rep", "dp"), None, None), P(None, "dp", None)
    return jax.shard_map(
        step,
        mesh=mesh,
        in_specs=(states, states) + (cut,) * 9,
        out_specs=(P("rep", "dp", None),) * 9,
        check_vma=False,
    )
```

profile of v0, /device:TPU:112, one launch (start us, length us, event | category | flops | bytes accessed | tf_op | source)
XLA Modules:
  0.0 621.5 jit_solution(11824896232564691047)
XLA Ops:
  7.2 0.0 copy-start.2
  7.2 0.1 all-gather.13.cloned.1.call-start
  7.3 2.8 fusion.88
  10.0 0.1 all-gather.13.cloned.1.call-update
  10.1 0.1 all-gather.15.cloned.1.call-start
  10.2 2.7 fusion.87
  12.8 0.1 all-gather.15.cloned.1.call-update
  12.9 0.1 all-gather.17.cloned.1.call-start
  13.0 1.3 fusion.86
  14.3 0.1 all-gather.17.cloned.1.call-update
  14.3 0.1 all-gather.21.cloned.1.call-start
  14.4 0.6 all-gather.21.cloned.1.call-update
  15.0 0.1 all-gather.23.cloned.1.call-start
  15.0 0.6 all-gather.23.cloned.1.call-update
  15.6 0.1 all-gather.19.cloned.1.call-start
  15.7 0.6 all-gather.19.cloned.1.call-update
  16.3 0.1 reduce-scatter.15.cloned.1.call-start
  16.3 6.5 %copy.20 = bf16[1,2048,1024]{1,2,0:T(8,128)(2,1)} copy(bf16[1,2048,1024]{2,1,0:T(8,128)(2,1)} %param.11) | data formatting | bytes 8388608 | tf_op args[0]
  22.8 3.1 fusion.15
  25.9 6.6 %copy.21 = bf16[1,2048,1024]{1,2,0:T(8,128)(2,1)} copy(bf16[1,2048,1024]{2,1,0:T(8,128)(2,1)} %param.12) | data formatting | bytes 8388608 | tf_op args[1]
  32.5 18.3 %all-gather.13.cloned.1.call-done = bf16[1,1024,3200]{2,1,0:T(8,128)(2,1)} async-done(((bf16[1,128,3200]{2,1,0:T(8,128)(2,1)}), bf16[1,1024,3200]{2,1,0:T(8,128)(2,1)}) %all-gather.13.cloned.1.call-update) | async-done | bytes 6553616 | tf_op jit(solution)/shard_map/all_gather | solution.py:35
  50.7 22.9 %fusion.41 = f32[2048,3200]{1,0:T(8,128)} fusion(bf16[1,1024,3200]{2,1,0:T(8,128)(2,1)} %all-gather.13.cloned.1.call-done, bf16[1,2048,1024]{1,2,0:T(8,128)(2,1)} %copy.20, f32[2048]{0:T(1024)S(1)} %add_rsqrt_fusion), kind=kOutput, calls=%fused_computation.59 | convolution fusion | flops 13428064256 | bytes 36970496 | tf_op jit(solution)/shard_map/dot_general | solution.py:21
  73.6 17.1 %all-gather.15.cloned.1.call-done = bf16[1,1024,3200]{2,1,0:T(8,128)(2,1)} async-done(((bf16[1,128,3200]{2,1,0:T(8,128)(2,1)}), bf16[1,1024,3200]{2,1,0:T(8,128)(2,1)}) %all-gather.15.cloned.1.call-update) | async-done | bytes 6553616 | tf_op jit(solution)/shard_map/all_gather | solution.py:35
  90.7 31.3 %multiply_convert_fusion.1 = (bf16[2048,3200]{1,0:T(8,128)(2,1)}, f32[2048,3200]{1,0:T(8,128)}) fusion(f32[2048,3200]{1,0:T(8,128)} %fusion.41, bf16[1,1024,3200]{2,1,0:T(8,128)(2,1)} %all-gather.15.cloned.1.call-done, bf16[1,2048,1024]{1,2,0:T(8,128)(2,1)} %copy.20, f32[2048]{0:T(1024)S(1)} %add_rsqrt_fusion), kind=kOutput, calls=%fused_computation.17 | convolution fusion | flops 13467385856 | bytes 76292096 | tf_op jit(solution)/shard_map/dot_general | solution.py:22
  122.1 8.6 %all-gather.17.cloned.1.call-done = bf16[1,3200,1024]{2,1,0:T(8,128)(2,1)} async-done(((bf16[1,400,1024]{2,1,0:T(8,128)(2,1)}), bf16[1,3200,1024]{2,1,0:T(8,128)(2,1)}) %all-gather.17.cloned.1.call-update) | async-done | bytes 6553616 | tf_op jit(solution)/shard_map/all_gather | solution.py:35
  130.7 21.8 %fusion.19 = (f32[2048]{0:T(1024)S(1)}, bf16[2048,1024]{0,1:T(8,128)(2,1)}) fusion(bf16[2048,3200]{1,0:T(8,128)(2,1)} %get-tuple-element.24, bf16[1,3200,1024]{2,1,0:T(8,128)(2,1)} %all-gather.17.cloned.1.call-done, bf16[1,2048,1024]{1,2,0:T(8,128)(2,1)} %copy.20), kind=kOutput, calls=%fused_computation.37 | convolution fusion | flops 13432256512 | bytes 28057600 | tf_op jit(solution)/shard_map/dot_general | solution.py:10
  152.5 18.0 %all-gather.21.cloned.1.call-done = bf16[1,3200,1024]{2,1,0:T(8,128)(2,1)} async-done(((bf16[1,400,1024]{2,1,0:T(8,128)(2,1)}), bf16[1,3200,1024]{2,1,0:T(8,128)(2,1)}) %all-gather.21.cloned.1.call-update) | async-done | bytes 6553616 | tf_op jit(solution)/shard_map/all_gather | solution.py:35
  170.5 20.9 %convolution_convert_fusion.1 = bf16[2048,3200]{1,0:T(8,128)(2,1)} fusion(bf16[1,3200,1024]{2,1,0:T(8,128)(2,1)} %all-gather.21.cloned.1.call-done, bf16[1,2048,1024]{2,1,0:T(8,128)(2,1)} %param.12), kind=kOutput, calls=%fused_computation.23 | convolution fusion | flops 13428326400 | bytes 23855104 | tf_op jit(solution)/shard_map/transpose(jvp())/dot_general | solution.py:10
  191.4 18.9 %all-gather.23.cloned.1.call-done = bf16[1,1024,3200]{2,1,0:T(8,128)(2,1)} async-done(((bf16[1,128,3200]{2,1,0:T(8,128)(2,1)}), bf16[1,1024,3200]{2,1,0:T(8,128)(2,1)}) %all-gather.23.cloned.1.call-update) | async-done | bytes 6553616 | tf_op jit(solution)/shard_map/all_gather | solution.py:35
  210.3 22.8 %fusion.28 = f32[2048,3200]{1,0:T(8,128)} fusion(bf16[1,1024,3200]{2,1,0:T(8,128)(2,1)} %all-gather.23.cloned.1.call-done, bf16[2048,1024]{0,1:T(8,128)(2,1)} %get-tuple-element.27, f32[2048]{0:T(1024)S(1)} %fusion.74), kind=kOutput, calls=%fused_computation.46 | convolution fusion | flops 13428064256 | bytes 36970496 | tf_op jit(solution)/shard_map/jvp()/dot_general | solution.py:22
  233.1 17.0 %all-gather.19.cloned.1.call-done = bf16[1,1024,3200]{2,1,0:T(8,128)(2,1)} async-done(((bf16[1,128,3200]{2,1,0:T(8,128)(2,1)}), bf16[1,1024,3200]{2,1,0:T(8,128)(2,1)}) %all-gather.19.cloned.1.call-update) | async-done | bytes 6553616 | tf_op jit(solution)/shard_map/all_gather | solution.py:35
  250.1 38.7 %fusion.2 = (bf16[2048,3200]{1,0:T(8,128)(2,1)}, f32[2048,3200]{1,0:T(8,128)}) fusion(f32[2048,3200]{1,0:T(8,128)} %fusion.28, bf16[2048,3200]{1,0:T(8,128)(2,1)} %convolution_convert_fusion.1, bf16[1,1024,3200]{2,1,0:T(8,128)(2,1)} %all-gather.19.cloned.1.call-done, bf16[2048,1024]{0,1:T(8,128)(2,1)} %get-tuple-element.27, f32[2048]{0:T(1024)S(1)} %fusion.74), kind=kOutput, calls=%fused_computation.8 | convolution fusion | flops 13506707456 | bytes 89399296 | tf_op jit(solution)/shard_map/jvp()/dot_general | solution.py:21
  288.8 22.6 %fusion.12 = bf16[2048,1024]{0,1:T(8,128)(2,1)} fusion(bf16[2048,3200]{1,0:T(8,128)(2,1)} %convolution_convert_fusion.1, bf16[1,1024,3200]{2,1,0:T(8,128)(2,1)} %all-gather.23.cloned.1.call-done, f32[2048,3200]{1,0:T(8,128)} %get-tuple-element.29), kind=kOutput, calls=%fused_computation.21 | convolution fusion | flops 13461094400 | bytes 50069504 | tf_op jit(solution)/shard_map/transpose(jvp())/dot_general | solution.py:22
  311.4 21.8 %fusion.21 = (f32[2048]{0:T(1024)S(1)}, bf16[2048,1024]{0,1:T(8,128)(2,1)}) fusion(bf16[2048,1024]{0,1:T(8,128)(2,1)S(1)} %copy-done.6, bf16[2048,1024]{0,1:T(8,128)(2,1)} %fusion.12, bf16[2048,3200]{1,0:T(8,128)(2,1)} %get-tuple-element.28, bf16[1,1024,3200]{2,1,0:T(8,128)(2,1)} %all-gather.19.cloned.1.call-done), kind=kOutput, calls=%fused_computation.39 | convolution fusion | flops 13432256512 | bytes 32251904 | tf_op jit(solution)/shard_map/transpose(jvp())/dot_general | solution.py:21
  333.3 4.9 fusion.44
  338.2 2.0 copy-done.7
  340.2 19.5 %convolution_convert_fusion.2 = bf16[3200,1024]{1,0:T(8,128)(2,1)} fusion(bf16[2048,3200]{1,0:T(8,128)(2,1)} %get-tuple-element.24, bf16[2048,1024]{0,1:T(8,128)(2,1)S(1)} %fusion.44), kind=kOutput, calls=%fused_computation.44 | convolution fusion | flops 13425049600 | bytes 23855104 | tf_op jit(solution)/shard_map/transpose(jvp())/dot_general | solution.py:10
  359.7 0.1 reduce-scatter.15.cloned.1.call-update
  359.8 0.1 reduce-scatter.17.cloned.1.call-start
  359.9 26.1 %fusion.25 = bf16[3200,1024]{1,0:T(8,128)(2,1)} fusion(f32[2048,3200]{1,0:T(8,128)} %fusion.28, bf16[1,2048,1024]{2,1,0:T(8,128)(2,1)} %param.12, f32[2048,3200]{1,0:T(8,128)} %get-tuple-element.29), kind=kOutput, calls=%fused_computation.41 | convolution fusion | flops 13464371200 | bytes 63176704 | tf_op jit(solution)/shard_map/transpose(jvp())/dot_general | solution.py:10
  386.0 0.1 reduce-scatter.17.cloned.1.call-update
  386.0 0.1 reduce-scatter.11.cloned.1.call-start
  386.1 21.4 %convolution_convert_fusion = bf16[2048,3200]{1,0:T(8,128)(2,1)} fusion(bf16[2048,1024]{0,1:T(8,128)(2,1)} %copy-done.7, bf16[1,3200,1024]{2,1,0:T(8,128)(2,1)} %all-gather.17.cloned.1.call-done), kind=kOutput, calls=%fused_computation.22 | convolution fusion | flops 13428326400 | bytes 23855104 | tf_op jit(solution)/shard_map/transpose(jvp())/dot_general | solution.py:10
  407.6 24.3 %fusion.27 = bf16[1024,3200]{1,0:T(8,128)(2,1)} fusion(bf16[2048,3200]{1,0:T(8,128)(2,1)} %convolution_convert_fusion, f32[2048,3200]{1,0:T(8,128)} %fusion.41, bf16[1,2048,1024]{1,2,0:T(8,128)(2,1)S(1)} %copy-done.1, f32[2048]{0:T(1024)S(1)} %copy-done.13), kind=kOutput, calls=%fused_computation.43 | convolution fusion | flops 13470662656 | bytes 50077696 | tf_op jit(solution)/shard_map/transpose(jvp())/dot_general | solution.py:22
  431.8 0.1 reduce-scatter.11.cloned.1.call-update
  431.9 0.1 reduce-scatter.13.cloned.1.call-start
  432.0 0.6 copy-done.9
  432.5 25.4 %fusion.26 = bf16[1024,3200]{1,0:T(8,128)(2,1)} fusion(bf16[2048,3200]{1,0:T(8,128)(2,1)} %convolution_convert_fusion.1, bf16[2048,1024]{0,1:T(8,128)(2,1)} %get-tuple-element.27, f32[2048]{0:T(1024)S(1)} %copy-done.9, f32[2048,3200]{1,0:T(8,128)} %get-tuple-element.29), kind=kOutput, calls=%fused_computation.42 | convolution fusion | flops 13470662656 | bytes 50077696 | tf_op jit(solution)/shard_map/transpose(jvp())/dot_general | solution.py:22
  457.9 0.1 reduce-scatter.13.cloned.1.call-update
  458.0 0.1 reduce-scatter.7.cloned.1.call-start
  458.0 32.5 %fusion.22 = bf16[1024,3200]{1,0:T(8,128)(2,1)} fusion(f32[2048,3200]{1,0:T(8,128)} %fusion.41, f32[2048,3200]{1,0:T(8,128)} %get-tuple-element.25, bf16[2048,3200]{1,0:T(8,128)(2,1)} %convolution_convert_fusion, bf16[1,2048,1024]{1,2,0:T(8,128)(2,1)} %copy.20, f32[2048]{0:T(1024)S(1)} %copy-done.13), kind=kOutput, calls=%fused_computation.40 | convolution fusion | flops 13503430656 | bytes 76292096 | tf_op jit(solution)/shard_map/transpose(jvp())/dot_general | solution.py:21
  490.6 0.1 reduce-scatter.7.cloned.1.call-update
  490.6 0.1 reduce-scatter.9.cloned.1.call-start
  490.7 21.0 %convolution_convert_fusion.3 = bf16[1024,3200]{1,0:T(8,128)(2,1)} fusion(bf16[2048,3200]{1,0:T(8,128)(2,1)} %get-tuple-element.28, bf16[2048,1024]{0,1:T(8,128)(2,1)} %get-tuple-element.27, f32[2048]{0:T(1024)S(1)} %copy-done.9), kind=kOutput, calls=%fused_computation.45 | convolution fusion | flops 13428064256 | bytes 23863296 | tf_op jit(solution)/shard_map/transpose(jvp())/dot_general | solution.py:21
  511.8 0.1 reduce-scatter.9.cloned.1.call-update
  511.8 0.0 reduce-scatter.15.cloned.1.call-done
  511.9 0.0 reduce-scatter.17.cloned.1.call-done
  511.9 1.3 copy-done.3
  513.2 6.5 %fusion.61 = (bf16[2,400,1024]{2,1,0:T(8,128)(2,1)}, f32[2,400,1024]{2,1,0:T(8,128)}, f32[2,400,1024]{2,1,0:T(8,128)}) fusion(bf16[2,400,1024]{2,1,0:T(8,128)(2,1)S(1)} %copy-done.3, bf16[1,400,1024]{2,1,0:T(8,128)(2,1)} %bitcast.67, bf16[1,400,1024]{2,1,0:T(8,128)(2,1)} %bitcast.66, f32[2,400,1024]{2,1,0:T(8,128)} %param.21, f32[2,400,1024]{2,1,0:T(8,128)} %param.18), kind=kLoop, calls=%fused_computation.88 | loop fusion | flops 15564800 | bytes 18022400 | tf_op jit(solution)/shard_map/convert_element_type | solution.py:30
  519.7 5.1 reduce-scatter.13.cloned.1.call-done
  524.8 6.5 %fusion.57 = (bf16[2,128,3200]{2,1,0:T(8,128)(2,1)}, f32[2,128,3200]{2,1,0:T(8,128)}, f32[2,128,3200]{2,1,0:T(8,128)}) fusion(bf16[2,128,3200]{2,1,0:T(8,128)(2,1)S(1)} %copy-done.4, bf16[1,128,3200]{2,1,0:T(8,128)(2,1)} %bitcast.69, bf16[1,128,3200]{2,1,0:T(8,128)(2,1)} %bitcast.68, f32[2,128,3200]{2,1,0:T(8,128)} %param.20, f32[2,128,3200]{2,1,0:T(8,128)} %param.17), kind=kLoop, calls=%fused_computation.84 | loop fusion | flops 15564800 | bytes 18022400 | tf_op jit(solution)/shard_map/convert_element_type | solution.py:30
  531.2 35.3 %reduce-scatter.7.cloned.1.call-done = bf16[128,3200]{1,0:T(8,128)(2,1)} async-done(((bf16[1024,3200]{1,0:T(8,128)(2,1)}), bf16[128,3200]{1,0:T(8,128)(2,1)}) %reduce-scatter.7.cloned.1.call-update) | async-done | bytes 819216 | tf_op jit(solution)/shard_map/reduce_scatter | solution.py:48
  566.5 41.6 %reduce-scatter.9.cloned.1.call-done = bf16[128,3200]{1,0:T(8,128)(2,1)} async-done(((bf16[1024,3200]{1,0:T(8,128)(2,1)}), bf16[128,3200]{1,0:T(8,128)(2,1)}) %reduce-scatter.9.cloned.1.call-update) | async-done | bytes 819216 | tf_op jit(solution)/shard_map/reduce_scatter | solution.py:48
  608.0 6.3 %fusion.53 = (bf16[2,128,3200]{2,1,0:T(8,128)(2,1)}, f32[2,128,3200]{2,1,0:T(8,128)}, f32[2,128,3200]{2,1,0:T(8,128)}) fusion(bf16[2,128,3200]{2,1,0:T(8,128)(2,1)S(1)} %copy-done.5, bf16[1,128,3200]{2,1,0:T(8,128)(2,1)} %bitcast.71, bf16[1,128,3200]{2,1,0:T(8,128)(2,1)} %bitcast.70, f32[2,128,3200]{2,1,0:T(8,128)} %param.19, f32[2,128,3200]{2,1,0:T(8,128)} %param.16), kind=kLoop, calls=%fused_computation.80 | loop fusion | flops 15564800 | bytes 18022400 | tf_op jit(solution)/shard_map/convert_element_type | solution.py:30
  (28 shorter events, 0.1 us)
Async XLA Ops:
  7.2 5.8 copy-start.2
  7.2 43.5 %all-gather.13.cloned.1.call-start = ((), (), s32[]{:S(2)}) async-start(), calls=%async_computation.12 | async-start | bytes 7372800 | tf_op jit(solution)/shard_map/all_gather | solution.py:35
  10.1 80.6 %all-gather.15.cloned.1.call-start = ((), (), s32[]{:S(2)}) async-start(), calls=%async_computation.13 | async-start | bytes 7372800 | tf_op jit(solution)/shard_map/all_gather | solution.py:35
  12.9 117.8 %all-gather.17.cloned.1.call-start = ((), (), s32[]{:S(2)}) async-start(), calls=%async_computation.14 | async-start | bytes 7372800 | tf_op jit(solution)/shard_map/all_gather | solution.py:35
  14.3 156.2 %all-gather.21.cloned.1.call-start = ((), (), s32[]{:S(2)}) async-start(), calls=%async_computation.16 | async-start | bytes 7372800 | tf_op jit(solution)/shard_map/all_gather | solution.py:35
  15.0 195.3 %all-gather.23.cloned.1.call-start = ((), (), s32[]{:S(2)}) async-start(), calls=%async_computation.17 | async-start | bytes 7372800 | tf_op jit(solution)/shard_map/all_gather | solution.py:35
  15.6 234.5 %all-gather.19.cloned.1.call-start = ((), (), s32[]{:S(2)}) async-start(), calls=%async_computation.15 | async-start | bytes 7372800 | tf_op jit(solution)/shard_map/all_gather | solution.py:35
  16.3 495.6 %reduce-scatter.15.cloned.1.call-start = ((), (), s32[]{:S(2)}) async-start(), calls=%async_computation.10 | async-start | bytes 7372800 | tf_op jit(solution)/shard_map/reduce_scatter | solution.py:48
  25.9 64.8 %copy-start.12 = (f32[2048]{0:T(1024)}, f32[2048]{0:T(1024)S(1)}, u32[]{:S(2)}) copy-start(f32[2048]{0:T(1024)S(1)} %add_rsqrt_fusion) | copy-start | bytes 24580
  152.5 38.9 %copy-start.10 = (f32[2048]{0:T(1024)}, f32[2048]{0:T(1024)S(1)}, u32[]{:S(2)}) copy-start(f32[2048]{0:T(1024)S(1)} %get-tuple-element.26) | copy-start | bytes 24580
  152.5 180.8 %copy-start.8 = (f32[2048]{0:T(1024)}, f32[2048]{0:T(1024)S(1)}, u32[]{:S(2)}) copy-start(f32[2048]{0:T(1024)S(1)} %fusion.74) | copy-start | bytes 24580
  288.8 22.6 %copy-start.6 = (bf16[2048,1024]{0,1:T(8,128)(2,1)S(1)}, bf16[2048,1024]{0,1:T(8,128)(2,1)}, u32[]{:S(2)}) copy-start(bf16[2048,1024]{0,1:T(8,128)(2,1)} %get-tuple-element.27) | copy-start | bytes 12582916
  311.4 21.8 %copy-start.11 = (f32[2048]{0:T(1024)S(1)}, f32[2048]{0:T(1024)}, u32[]{:S(2)}) copy-start(f32[2048]{0:T(1024)} %copy-done.10) | copy-start | bytes 24580
  311.4 21.9 %copy-start = (bf16[1,2048,1024]{1,2,0:T(8,128)(2,1)S(1)}, bf16[1,2048,1024]{1,2,0:T(8,128)(2,1)}, u32[]{:S(2)}) copy-start(bf16[1,2048,1024]{1,2,0:T(8,128)(2,1)} %copy.21) | copy-start | bytes 12582916
  338.2 2.0 copy-start.7
  359.8 152.1 %reduce-scatter.17.cloned.1.call-start = ((), (), s32[]{:S(2)}) async-start(), calls=%async_computation.11 | async-start | bytes 7372800 | tf_op jit(solution)/shard_map/reduce_scatter | solution.py:48
  386.0 21.5 %copy-start.13 = (f32[2048]{0:T(1024)S(1)}, f32[2048]{0:T(1024)}, u32[]{:S(2)}) copy-start(f32[2048]{0:T(1024)} %copy-done.12) | copy-start | bytes 24580
  386.0 133.7 %reduce-scatter.11.cloned.1.call-start = ((), (), s32[]{:S(2)}) async-start(), calls=%async_computation.8 | async-start | bytes 7372800 | tf_op jit(solution)/shard_map/reduce_scatter | solution.py:48
  386.1 21.4 %copy-start.1 = (bf16[1,2048,1024]{1,2,0:T(8,128)(2,1)S(1)}, bf16[1,2048,1024]{1,2,0:T(8,128)(2,1)}, u32[]{:S(2)}) copy-start(bf16[1,2048,1024]{1,2,0:T(8,128)(2,1)} %copy.20) | copy-start | bytes 12582916
  431.8 0.7 copy-start.9
  431.9 92.9 %reduce-scatter.13.cloned.1.call-start = ((), (), s32[]{:S(2)}) async-start(), calls=%async_computation.9 | async-start | bytes 7372800 | tf_op jit(solution)/shard_map/reduce_scatter | solution.py:48
  458.0 108.5 %reduce-scatter.7.cloned.1.call-start = ((), (), s32[]{:S(2)}) async-start(), calls=%async_computation.6 | async-start | bytes 7372800 | tf_op jit(solution)/shard_map/reduce_scatter | solution.py:48
  490.6 117.4 %reduce-scatter.9.cloned.1.call-start = ((), (), s32[]{:S(2)}) async-start(), calls=%async_computation.7 | async-start | bytes 7372800 | tf_op jit(solution)/shard_map/reduce_scatter | solution.py:48
  511.8 1.4 copy-start.3
  513.2 11.6 %copy-start.4 = (bf16[2,128,3200]{2,1,0:T(8,128)(2,1)S(1)}, bf16[2,128,3200]{2,1,0:T(8,128)(2,1)}, u32[]{:S(2)}) copy-start(bf16[2,128,3200]{2,1,0:T(8,128)(2,1)} %param.14) | copy-start | bytes 4915204
  524.8 83.3 %copy-start.5 = (bf16[2,128,3200]{2,1,0:T(8,128)(2,1)S(1)}, bf16[2,128,3200]{2,1,0:T(8,128)(2,1)}, u32[]{:S(2)}) copy-start(bf16[2,128,3200]{2,1,0:T(8,128)(2,1)} %param.13) | copy-start | bytes 4915204
Sparse Core Ops, SparseCore 0:
  10.2 40.4 all-gather.12
  52.9 37.7 all-gather.14
  92.9 37.7 all-gather.16
  132.7 37.7 all-gather.20
  172.5 37.7 all-gather.22
  212.3 37.7 all-gather.18
  359.9 39.8 reduce-scatter.14
  402.1 39.3 reduce-scatter.16
  443.8 39.3 reduce-scatter.10
  485.4 39.3 reduce-scatter.12
  527.1 39.3 reduce-scatter.6
  568.6 39.3 reduce-scatter.8
where the time goes:
time: 629 us; the launch traced here: 621 us
  matrix products  373 us (59%)
  waiting for transfers between devices  182 us (29%)
  other arithmetic  27.3 us (4%)
  local copies, waits for them, and re-layouts  23.7 us (4%)
  between operations  14.6 us (2%)
    dot_general x5, matrix products, layer(): gate = jnp.dot(a, w['w_gate'], preferred_element_type=jnp.float32)  137 us
    dot_general x5, matrix products, layer(): up = jnp.dot(a, w['w_up'], preferred_element_type=jnp.float32)  126 us
    dot_general x5, matrix products, matmul(): jnp.dot(a, w, preferred_element_type=jnp.float32).astype(jnp.bfloat16)  110 us
    all_gather x6, waiting for transfers between devices, fetched(): lax.all_gather(w[number], 'dp', axis=0, tiled=True)  97.9 us
    reduce_scatter x6, waiting for transfers between devices, step(): lax.psum_scatter(by_w[name], 'dp', scatter_dimension=0, tiled=True)  81.9 us
    convert_element_type x3, other arithmetic, adamw(): return ((w - 0.02 * step).astype(jnp.bfloat16), m, v)  19.3 us
    unnamed x30, local copies, waits for them, and re-layouts  17 us
  transfers between devices with their start and end apart: 12, of which 9 were waited for; matrix products, arithmetic and copies ran while one was open for 49% of the time, Pallas kernels for 0%

commit v1 on v0

v1 whole, which is shorter than its diff:
```python
import functools

import jax
import jax.numpy as jnp
from jax import lax
from jax.experimental import pallas as pl
from jax.experimental.pallas import tpu as pltpu
from jax.sharding import PartitionSpec as P

MESH = pl.DeviceIdType.MESH
F32, BF16 = jnp.float32, jnp.bfloat16
ANY = pl.BlockSpec(memory_space=pl.ANY)
BM = 256
MB = 2**20


def dot(a, b, ca=1, cb=0):
    return lax.dot_general(a, b, (((ca,), (cb,)), ((), ())), preferred_element_type=F32)


def normed(wide):
    scale = lax.rsqrt(jnp.mean(wide * wide, -1, keepdims=True) + 1e-6)
    return (wide * scale).astype(BF16)


def thirds(n, unit):
    tiles = n // unit
    side = tiles // 3
    return side * unit, (tiles - 2 * side) * unit, side * unit


def cuts(n):
    k = max(1, n // 512)
    return [(512 * j, 512 if j < k - 1 else n - 512 * j) for j in range(k)]


def fwd_kernel(
    x_ref, wg_ref, wu_ref, wd_ref,
    WG, WU, WD, G, U, H, A, h1_ref,
    sg, su, sd, a_v, x_v, hid_v, bg, bu, wd_v, st_g, st_u,
    io, ld, out_s, loc, own_s, own_r, rx_s, rx_r, dd_s, dd_r, pp_s, pp_r, pd_s, pd_r,
):
    tokens, d = x_v.shape
    steps = tokens // BM
    rep, me = lax.axis_index("rep"), lax.axis_index("dp")
    chips = 4
    xx, c = me // 2, lax.rem(me, 2)
    right = lax.rem(xx + 1, chips) * 2 + c
    left = lax.rem(xx + chips - 1, chips) * 2 + c
    opp = lax.rem(xx + 2, chips) * 2 + c
    core = xx * 2 + (1 - c)
    p = lax.rem(rep, 2)
    pair = rep + 1 - 2 * p
    to_right, to_left, to_core = {"dp": right}, {"dp": left}, {"dp": core}
    to_pair = {"rep": pair}
    others = [lax.rem(xx + k, chips) * 2 + (1 - c) for k in (chips - 1, 1, 2, 2)]
    mine = [left, right, opp, opp]

    shards = {"g": sg, "u": su, "d": sd}
    inputs = {"g": wg_ref, "u": wu_ref, "d": wd_ref}
    whole = {"g": WG, "u": WU, "d": WD}
    order = [("g", 0), ("u", 0), ("d", 0), ("g", 1), ("u", 1), ("d", 1)]
    number = {key: k for k, key in enumerate(order)}
    ring = [("g", 0, 0), ("u", 0, 0), ("g", 0, 1), ("u", 0, 1), ("d", 0, 0), ("d", 0, 1),
            ("g", 1, 0), ("u", 1, 0), ("g", 1, 1), ("u", 1, 1), ("d", 1, 0), ("d", 1, 1)]

    def extent(kind, pos):
        rows, cols = shards[kind].shape[1:]
        n, unit = (rows, 16) if kind == "d" else (cols, 128)
        w = thirds(n, unit)
        far = n - w[2]
        off = (p * far, w[0], (1 - p) * far)[pos]
        if pos != 1:
            off = pl.multiple_of(off, unit)
        return (off, w[pos], 0, cols) if kind == "d" else (0, rows, off, w[pos])

    def region(ref, kind, layer, pos, base, half=None):
        r0, rows, c0, cols = extent(kind, pos)
        if half is not None:
            first = (rows // 2 + 15) // 16 * 16
            r0, rows = (r0, first) if half == 0 else (r0 + first, rows - first)
        start = r0 + base
        if not isinstance(start, int):
            start = pl.multiple_of(start, 16)
        return ref.at[layer, pl.ds(start, rows), pl.ds(c0, cols)]

    def place(kind, layer, pos, shard, half=None):
        return region(whole[kind], kind, layer, pos, shard * shards[kind].shape[1], half)

    def remote(src, dst, ss, rs, to):
        return pltpu.make_async_remote_copy(src_ref=src, dst_ref=dst, send_sem=ss, recv_sem=rs, device_id=to, device_id_type=MESH)

    def got(dst, ss, rs):
        remote(dst, dst, ss, rs, to_core).wait_recv()

    HALF = (None, None, 0, 1)

    def send_ring(k, j):
        kind, layer, pos = ring[k]
        if j < 2:
            src = region(shards[kind], kind, layer, pos, 0)
            dst = place(kind, layer, pos, me)
            return remote(src, dst, rx_s.at[k, j], rx_r.at[k, j], (to_right, to_left)[j])
        shard = (left, right)[j - 2]
        at = place(kind, layer, pos, shard, j - 2)
        return remote(at, at, rx_s.at[k, j], rx_r.at[k, j], (to_right, to_left)[j - 2])

    def recv_ring(k, j):
        kind, layer, pos = ring[k]
        got(place(kind, layer, pos, mine[j], HALF[j]), rx_s.at[k, j], rx_r.at[k, j])

    def send_core(k, j):
        kind, layer, pos = ring[k]
        at = place(kind, layer, pos, mine[j], HALF[j])
        return remote(at, at, dd_s.at[k, j], dd_r.at[k, j], to_core)

    def recv_core(k, j):
        kind, layer, pos = ring[k]
        got(place(kind, layer, pos, others[j], HALF[j]), dd_s.at[k, j], dd_r.at[k, j])

    def send_pair(k, j):
        kind, layer, pos = ring[k]
        q = number[kind, layer]
        at = place(kind, layer, pos, mine[j], HALF[j])
        return remote(at, at, pp_s.at[q, j], pp_r.at[q, j], to_pair)

    def recv_pair(q, j):
        kind, layer = order[q]
        got(place(kind, layer, 2, mine[j], HALF[j]), pp_s.at[q, j], pp_r.at[q, j])

    def send_pair_core(q, j):
        kind, layer = order[q]
        at = place(kind, layer, 2, mine[j], HALF[j])
        return remote(at, at, pd_s.at[q, j], pd_r.at[q, j], to_core)

    def recv_pair_core(q, j):
        kind, layer = order[q]
        got(place(kind, layer, 2, others[j], HALF[j]), pd_s.at[q, j], pd_r.at[q, j])

    def slot_of(kind, layer, shard):
        rows = shards[kind].shape[1]
        return whole[kind].at[layer, pl.ds(pl.multiple_of(shard * rows, 16), rows), :]

    def send_own(q):
        kind, layer = order[q]
        return remote(shards[kind].at[layer], slot_of(kind, layer, me), own_s.at[q], own_r.at[q], to_core)

    def recv_own(q):
        kind, layer = order[q]
        got(slot_of(kind, layer, core), own_s.at[q], own_r.at[q])

    def keep_own(q):
        kind, layer = order[q]
        return pltpu.make_async_copy(shards[kind].at[layer], slot_of(kind, layer, me), loc.at[q])

    def I(k):
        for j in (0, 1):
            send_ring(k, j).start()

    def onward(k, j):
        send_core(k, j).start()
        if ring[k][2] == 0:
            send_pair(k, j).start()

    def Fw(k):
        for j in (0, 1):
            recv_ring(k, j)
            send_ring(k, 2 + j).start()
            onward(k, j)

    def Gw(k):
        for j in (2, 3):
            recv_ring(k, j)
            onward(k, j)

    def Hw(q):
        for j in range(4):
            recv_pair(q, j)
            send_pair_core(q, j).start()

    def whole_piece(kind, layer, pos):
        if pos == 2:
            for j in range(4):
                recv_pair_core(number[kind, layer], j)
        else:
            for j in range(4):
                recv_core(ring.index((kind, layer, pos)), j)

    first = [pltpu.make_async_copy(inputs[kind], shards[kind], io.at[n]) for n, kind in enumerate("gud")]
    for copy in first:
        copy.start()
    load_x = pltpu.make_async_copy(x_ref, x_v, io.at[3])
    load_x.start()
    barrier = pltpu.get_barrier_semaphore()
    for to in (to_right, to_left, to_core, to_pair):
        pl.semaphore_signal(barrier, inc=1, device_id=to, device_id_type=MESH)
    pl.semaphore_wait(barrier, 4)
    for copy in first:
        copy.wait()
    I(0)
    I(1)
    for q in (0, 1):
        send_own(q).start()
        keep_own(q).start()
    load_x.wait()

    @pl.loop(0, steps)
    def _(m):
        rows = pl.ds(pl.multiple_of(m * BM, BM), BM)
        a_v[rows, :] = normed(x_v[rows, :].astype(F32))

    keep_a = [pltpu.make_async_copy(a_v, A.at[layer], io.at[4 + layer]) for layer in range(2)]
    keep_a[0].start()
    Fw(0)
    I(2)
    Fw(1)
    Gw(0)
    I(3)
    Gw(1)
    for q in range(2, 6):
        send_own(q).start()
        keep_own(q).start()
    for q in (0, 1):
        keep_own(q).wait()
        recv_own(q)

    widths = thirds(wg_ref.shape[2], 128)
    starts = (0, widths[0], widths[0] + widths[1])

    def load_weights(layer, pos):
        _, _, c0, cols = extent("g", pos)
        slot = pos % 2
        return [
            pltpu.make_async_copy(w.at[layer, :, pl.ds(c0, cols)], b.at[slot, :, pl.ds(0, cols)], ld.at[slot, n])
            for n, (w, b) in enumerate(((WG, bg), (WU, bu)))
        ]

    def store_out(layer, pos, m):
        _, _, c0, cols = extent("g", pos)
        slot = lax.rem(m, 2)
        rows = pl.ds(pl.multiple_of(m * BM, BM), BM)
        return [
            pltpu.make_async_copy(st_g.at[slot, :, pl.ds(0, cols)], G.at[layer, rows, pl.ds(c0, cols)], out_s.at[slot, 0]),
            pltpu.make_async_copy(st_u.at[slot, :, pl.ds(0, cols)], U.at[layer, rows, pl.ds(c0, cols)], out_s.at[slot, 1]),
            pltpu.make_async_copy(hid_v.at[rows, pl.ds(starts[pos], cols)], H.at[layer, rows, pl.ds(c0, cols)], out_s.at[slot, 2]),
        ]

    def gate_up(layer, pos, acts):
        cols = widths[pos]
        slot = pos % 2
        for copy in load_weights(layer, pos):
            copy.wait()

        @pl.loop(0, steps)
        def _(m):
            for at, todo in acts.items():

                @pl.when(m == at)
                def _():
                    for act in todo:
                        act()

            rows = pl.ds(pl.multiple_of(m * BM, BM), BM)
            back = lax.rem(m, 2)

            @pl.when(m >= 2)
            def _():
                for copy in store_out(layer, pos, m - 2):
                    copy.wait()

            if pos:

                @pl.when(m < 2)
                def _():
                    for copy in store_out(layer, pos - 1, m + steps - 2):
                        copy.wait()

            a = a_v[rows, :]
            for c0, w in cuts(cols):
                gate = dot(a, bg[slot, :, c0 : c0 + w])
                up = dot(a, bu[slot, :, c0 : c0 + w])
                st_g[back, :, c0 : c0 + w] = gate
                st_u[back, :, c0 : c0 + w] = up
                hid_v[rows, starts[pos] + c0 : starts[pos] + c0 + w] = (gate * jax.nn.sigmoid(gate) * up).astype(BF16)
            for copy in store_out(layer, pos, m):
                copy.start()

        if pos == 2:
            for m in (steps - 2, steps - 1):
                for copy in store_out(layer, pos, m):
                    copy.wait()

    def ready(layer, pos):
        def act():
            for kind in "gu":
                whole_piece(kind, layer, pos)
            for copy in load_weights(layer, pos):
                copy.start()

        return act

    def then(*acts):
        for act in acts:
            act()

    P_ = functools.partial
    ready(0, 0)()
    gate_up(0, 0, {3: [P_(Fw, 2), P_(I, 4)], 6: [P_(Gw, 2)]})
    then(P_(Fw, 3), P_(I, 5), P_(Gw, 3), ready(0, 1))
    gate_up(0, 1, {0: [P_(Hw, 0)], 3: [P_(Fw, 4), P_(I, 6), P_(Hw, 1)], 6: [P_(Gw, 4)], 7: [ready(0, 2)]})
    gate_up(0, 2, {1: [P_(Fw, 5), P_(I, 7)], 4: [P_(Gw, 5)]})

    load_wd = []
    for n in range(3):
        _, _, c0, cols = extent("g", n)
        load_wd.append(pltpu.make_async_copy(WD.at[0, pl.ds(c0, cols), :], wd_v.at[pl.ds(starts[n], cols), :], io.at[6 + n]))
    Hw(2)
    keep_own(2).wait()
    recv_own(2)
    for pos in (0, 1, 2):
        whole_piece("d", 0, pos)
    for copy in load_wd:
        copy.start()
    then(P_(Fw, 6), P_(I, 8))
    keep_a[0].wait()
    for copy in load_wd:
        copy.wait()

    def own_1():
        for q in (3, 4):
            keep_own(q).wait()
            recv_own(q)

    acts = {1: [P_(Gw, 6)], 4: [P_(Fw, 7), P_(I, 9)], 6: [P_(Gw, 7)], 7: [own_1, ready(1, 0)]}

    @pl.loop(0, steps)
    def _(m):
        for at, todo in acts.items():

            @pl.when(m == at)
            def _():
                for act in todo:
                    act()

        rows = pl.ds(pl.multiple_of(m * BM, BM), BM)
        h = x_v[rows, :] + dot(hid_v[rows, :], wd_v[...]).astype(BF16)
        x_v[rows, :] = h
        a_v[rows, :] = normed(h.astype(F32))

    keep_h = pltpu.make_async_copy(x_v, h1_ref, io.at[9])
    keep_h.start()
    keep_a[1].start()
    gate_up(1, 0, {1: [P_(Fw, 8), P_(I, 10)], 3: [P_(Gw, 8), P_(Hw, 3)]})
    then(P_(Fw, 9), P_(I, 11), P_(Gw, 9), ready(1, 1))
    gate_up(1, 1, {3: [P_(Fw, 10)], 5: [P_(Gw, 10), P_(Hw, 4)], 7: [ready(1, 2)]})
    gate_up(1, 2, {2: [P_(Fw, 11)], 4: [P_(Gw, 11)]})
    Hw(5)
    keep_own(5).wait()
    recv_own(5)
    for pos in (0, 1, 2):
        whole_piece("d", 1, pos)
    keep_h.wait()
    keep_a[1].wait()
    for k in range(len(ring)):
        for j in range(4):
            send_ring(k, j).wait_send()
            send_core(k, j).wait_send()
            if ring[k][2] == 0:
                send_pair(k, j).wait_send()
    for q in range(len(order)):
        send_own(q).wait_send()
        for j in range(4):
            send_pair_core(q, j).wait_send()


def forward(x, wg, wu, wd):
    tokens, d = x.shape
    layers, _, ff = wg.shape
    dma = lambda *s: pltpu.SemaphoreType.DMA(s)
    big = max(thirds(ff, 128))
    like = lambda s, t=BF16: jax.ShapeDtypeStruct(s, t)
    return pl.pallas_call(
        fwd_kernel,
        name="forward",
        in_specs=[ANY] * 4,
        out_specs=[ANY] * 8,
        out_shape=[
            like((layers, d, ff)), like((layers, d, ff)), like((layers, ff, d)),
            like((layers, tokens, ff), F32), like((layers, tokens, ff), F32), like((layers, tokens, ff)),
            like((layers, tokens, d)), like((tokens, d)),
        ],
        scratch_shapes=[
            pltpu.VMEM(wg.shape, BF16), pltpu.VMEM(wu.shape, BF16), pltpu.VMEM(wd.shape, BF16),
            pltpu.VMEM((tokens, d), BF16), pltpu.VMEM((tokens, d), BF16), pltpu.VMEM((tokens, ff), BF16),
            pltpu.VMEM((2, d, big), BF16), pltpu.VMEM((2, d, big), BF16), pltpu.VMEM((ff, d), BF16),
            pltpu.VMEM((2, BM, big), F32), pltpu.VMEM((2, BM, big), F32),
            dma(10), dma(2, 2), dma(2, 3), dma(6), dma(6), dma(6), dma(12, 4), dma(12, 4), dma(12, 4), dma(12, 4),
            dma(6, 4), dma(6, 4), dma(6, 4), dma(6, 4),
        ],
        compiler_params=pltpu.CompilerParams(collective_id=0, has_side_effects=True, vmem_limit_bytes=64 * MB - 64 * 1024),
        cost_estimate=pl.CostEstimate(flops=10 * tokens * d * ff, bytes_accessed=200 * MB, transcendentals=0),
    )(x, wg, wu, wd)


def call(body, name, grid, in_specs, out_specs, out_shape, mats):
    return pl.pallas_call(
        body,
        name=name,
        grid=grid,
        in_specs=in_specs,
        out_specs=out_specs,
        out_shape=out_shape,
        compiler_params=pltpu.CompilerParams(vmem_limit_bytes=60 * MB),
        cost_estimate=pl.CostEstimate(flops=int(mats * 2 * 2048 * 1024 * 3200), bytes_accessed=20 * MB, transcendentals=0),
    )


def by_weight(a, b, layer, bm, bn, name):
    tokens, m = a.shape[-2:]
    n = b.shape[-1]

    def body(a_ref, b_ref, o_ref):
        o_ref[...] = dot(a_ref[...].reshape(tokens, bm), b_ref[...], 0, 0).astype(BF16)

    spec = pl.BlockSpec((None, tokens, bm), lambda j, i: (layer, 0, i)) if a.ndim == 3 else pl.BlockSpec((tokens, bm), lambda j, i: (0, i))
    return call(
        body, name, (n // bn, m // bm), [spec, pl.BlockSpec((tokens, bn), lambda j, i: (0, j))],
        pl.BlockSpec((bm, bn), lambda j, i: (i, j)), jax.ShapeDtypeStruct((m, n), BF16), 1,
    )(a, b)


def by_gates(by_h, WD, G, U, layer, name):
    tokens, d = by_h.shape
    ff = WD.shape[1]
    bm, bn = 512, 640

    def body(by_ref, w_ref, g_ref, u_ref, dg_ref, du_ref):
        by = by_ref[...]
        for c0, w in cuts(bn):
            dh = dot(by, w_ref[c0 : c0 + w, :], 1, 1).astype(BF16).astype(F32)
            gate, up = g_ref[:, c0 : c0 + w], u_ref[:, c0 : c0 + w]
            sig = jax.nn.sigmoid(gate)
            silu = gate * sig
            du_ref[:, c0 : c0 + w] = (dh * silu).astype(BF16)
            dg_ref[:, c0 : c0 + w] = (dh * up * (sig + silu * (1 - sig))).astype(BF16)

    wide = pl.BlockSpec((None, bm, bn), lambda j, i: (layer, i, j))
    out = pl.BlockSpec((bm, bn), lambda j, i: (i, j))
    return call(
        body, name, (ff // bn, tokens // bm),
        [pl.BlockSpec((bm, d), lambda j, i: (i, 0)), pl.BlockSpec((None, bn, d), lambda j, i: (layer, j, 0)), wide, wide],
        [out, out], [jax.ShapeDtypeStruct((tokens, ff), BF16)] * 2, 1,
    )(by_h, WD, G, U)


def by_states(dg, du, WG, WU, h, by_h, layer, name):
    tokens, ff = dg.shape
    d = h.shape[1]
    bm = 256

    def body(dg_ref, du_ref, wg_ref, wu_ref, h_ref, by_ref, o_ref):
        da = dot(dg_ref[...], wg_ref[...], 1, 1).astype(BF16).astype(F32) + dot(du_ref[...], wu_ref[...], 1, 1).astype(BF16).astype(F32)
        da = da.astype(BF16).astype(F32)
        wide = h_ref[...].astype(F32)
        scale = lax.rsqrt(jnp.mean(wide * wide, -1, keepdims=True) + 1e-6)
        along = jnp.mean(da * wide, -1, keepdims=True)
        by = da * scale - wide * (scale * scale * scale * along)
        o_ref[...] = by_ref[...] + by.astype(BF16)

    rows = pl.BlockSpec((bm, ff), lambda i: (i, 0))
    full = pl.BlockSpec((None, d, ff), lambda i: (layer, 0, 0))
    out = pl.BlockSpec((bm, d), lambda i: (i, 0))
    return call(body, name, (tokens // bm,), [rows, rows, full, full, out, out], out, jax.ShapeDtypeStruct((tokens, d), BF16), 2)(
        dg, du, WG, WU, h, by_h
    )


def adamw(w, m, v, g):
    m = 0.9 * m + 0.1 * g
    v = 0.95 * v + 0.05 * g * g
    step = m * lax.rsqrt(v + 1e-8) + 0.1 * w
    return (w - 0.02 * step).astype(jnp.bfloat16), m, v


def solution(mesh):
    def step(x, dy, *arrays):
        weights, m, v = (arrays[i : i + 3] for i in (0, 3, 6))
        x, dy = x[0], dy[0]
        WG, WU, WD, G, U, H, A, h1 = forward(x, *weights)
        scatter = lambda g: lax.psum_scatter(g, "dp", scatter_dimension=0, tiled=True)
        d1 = scatter(by_weight(H, dy, 1, 640, 1024, "dw_down1"))
        dg, du = by_gates(dy, WD, G, U, 1, "gates1")
        g1 = scatter(by_weight(A, dg, 1, 1024, 640, "dw_gate1"))
        u1 = scatter(by_weight(A, du, 1, 1024, 640, "dw_up1"))
        by_h = by_states(dg, du, WG, WU, h1, dy, 1, "states1")
        d0 = scatter(by_weight(H, by_h, 0, 640, 1024, "dw_down0"))
        dg, du = by_gates(by_h, WD, G, U, 0, "gates0")
        g0 = scatter(by_weight(A, dg, 0, 1024, 640, "dw_gate0"))
        u0 = scatter(by_weight(A, du, 0, 1024, 640, "dw_up0"))
        gradients = [jnp.stack(pair).astype(F32) for pair in ((g0, g1), (u0, u1), (d0, d1))]
        new = [adamw(w.astype(F32), m, v, g) for w, m, v, g in zip(weights, m, v, gradients, strict=True)]
        return tuple(one[which] for which in range(3) for one in new)

    states, cut = P(("rep", "dp"), None, None), P(None, "dp", None)
    return jax.shard_map(
        step,
        mesh=mesh,
        in_specs=(states, states) + (cut,) * 9,
        out_specs=(P("rep", "dp", None),) * 9,
        check_vma=False,
    )
```

time: 629 us -> 546 us (0.87); the launches traced: 621 us -> 546 us
  Pallas kernels: 0 us -> 426 us
  matrix products: 373 us -> 0 us
  waiting for transfers between devices: 182 us -> 84.2 us
  local copies, waits for them, and re-layouts: 23.7 us -> 1.81 us
  other arithmetic: 27.3 us -> 19 us
    pallas_call x0 -> x10, Pallas kernels: none -> 426 us  [the longest x1 172 us: forward(): pl.pallas_call(fwd_kernel, name='forward', in_specs=[ANY] * 4, out_specs=...]
    dot_general x15 -> x0, matrix products: 373 us -> none  [the longest x5 137 us: layer(): gate = jnp.dot(a, w['w_gate'], preferred_element_type=jnp.float32)]
    all_gather x6 -> x0, waiting for transfers between devices: 97.9 us -> none  [fetched(): lax.all_gather(w[number], 'dp', axis=0, tiled=True)]
    unnamed x30 -> x4, local copies, waits for them, and re-layouts: 17 us -> 1.81 us
    slice x3 -> x0, local copies, waits for them, and re-layouts: 6.73 us -> none  [fetched(): w[number]]
  transfers between devices with their start and end apart: 12 -> 6, of which waited for: 9 -> 3; matrix products, arithmetic and copies ran while one was open for 49% -> 2% of each run, Pallas kernels for 0% -> 28%
where the time goes in v1:
time: 546 us
  Pallas kernels  426 us (78%)
  waiting for transfers between devices  84.2 us (15%)
  other arithmetic  19 us (3%)
  between operations  14.2 us (3%)
    pallas_call x1, Pallas kernels, forward(): pl.pallas_call(fwd_kernel, name='forward', in_specs=[ANY] * 4, out_specs=...  172 us
    pallas_call x6, Pallas kernels, by_weight(): call(body, name, (n // bn, m // bm), [spec, pl.BlockSpec((tokens, bn), la...  124 us
    pallas_call x2, Pallas kernels, by_gates(): call(body, name, (ff // bn, tokens // bm), [pl.BlockSpec((bm, d), lambda...  91 us
    reduce_scatter x6, waiting for transfers between devices, step(): lax.psum_scatter(g, 'dp', scatter_dimension=0, tiled=True)  83.9 us
    pallas_call x1, Pallas kernels, by_states(): call(body, name, (tokens // bm,), [rows, rows, full, full, out, out], out...  39.5 us
    convert_element_type x3, other arithmetic, adamw(): return ((w - 0.02 * step).astype(jnp.bfloat16), m, v)  19 us
  transfers between devices with their start and end apart: 6, of which 3 were waited for; matrix products, arithmetic and copies ran while one was open for 2% of the time, Pallas kernels for 28%

profile of v1, /device:TPU:112, one launch (start us, length us, event | category | flops | bytes accessed | tf_op | source)
XLA Modules:
  0.0 546.1 jit_solution(7776052590145703807)
XLA Ops:
  7.2 0.1 reduce-scatter.15.cloned.1.call-start
  7.3 171.8 %forward.1 = (bf16[2,1024,3200]{2,1,0:T(8,128)(2,1)}, bf16[2,1024,3200]{2,1,0:T(8,128)(2,1)}, bf16[2,3200,1024]{2,1,0:T(8,128)(2,1)}, f32[2,2048,3200]{2,1,0:T(8...) custom-call(bf16[2048,1024]{1,0:T(8,128)(2,1)} %bitcast.17, ...), custom_call_target="tpu_custom_call" | custom-call | flops 67108864000 | bytes 209715200 | tf_op jit(solution)/shard_map/forward/pallas_call | solution.py:382
  179.1 45.5 %gates1.1 = (bf16[2048,3200]{1,0:T(8,128)(2,1)}, bf16[2048,3200]{1,0:T(8,128)(2,1)}) custom-call(bf16[2048,1024]{1,0:T(8,128)(2,1)} %bitcast.8, bf16[2,3200,1024]{2,1,0:T(8,128)(2,1)} %get-tuple-element.22.w_ref, f32[2,2048,3200]{2,1,0:T(8,128)} %get-tuple-element.23.g_ref, f32[2,2048,3200]{2,1,0:T(8,128)} %get-tuple-element.24.u_ref), custom_call_target="tpu_custom_call" | custom-call | flops 13421772800 | bytes 20971520 | tf_op jit(solution)/shard_map/gates1/pallas_call | solution.py:449
  224.6 39.5 %states1.1.by_ref.b_ref = bf16[2048,1024]{1,0:T(8,128)(2,1)} custom-call(bf16[2048,3200]{1,0:T(8,128)(2,1)} %get-tuple-element.25.dg_ref.b_ref, bf16[2048,3200]{1,0:T(8,128)(2,1)} %get-tuple-element.26.du_ref.b_ref, bf16[2,1024,3200]{2,1,0:T(8,128)(2,1)} %get-tuple-element.27.wg_ref, bf16[2,1024,3200]{2,1,0:T(8,128)(2,1)} %get-tuple-element.28.wu_ref, ...), custom_call_target="tpu_custom_call" | custom-call | flops 26843545600 | bytes 20971520 | tf_op jit(solution)/shard_map/states1/pallas_call | solution.py:473
  264.1 18.6 %dw_down0.1 = bf16[3200,1024]{1,0:T(8,128)(2,1)} custom-call(bf16[2,2048,3200]{2,1,0:T(8,128)(2,1)} %get-tuple-element.32.a_ref, bf16[2048,1024]{1,0:T(8,128)(2,1)} %states1.1.by_ref.b_ref), custom_call_target="tpu_custom_call" | custom-call | flops 13421772800 | bytes 20971520 | tf_op jit(solution)/shard_map/dw_down0/pallas_call | solution.py:426
  282.7 0.1 reduce-scatter.15.cloned.1.call-update
  282.8 0.1 reduce-scatter.17.cloned.1.call-start
  282.9 18.7 %dw_down1.1 = bf16[3200,1024]{1,0:T(8,128)(2,1)} custom-call(bf16[2,2048,3200]{2,1,0:T(8,128)(2,1)} %get-tuple-element.32.a_ref, bf16[2048,1024]{1,0:T(8,128)(2,1)} %bitcast.10), custom_call_target="tpu_custom_call" | custom-call | flops 13421772800 | bytes 20971520 | tf_op jit(solution)/shard_map/dw_down1/pallas_call | solution.py:426
  301.5 0.1 reduce-scatter.17.cloned.1.call-update
  301.6 0.1 reduce-scatter.11.cloned.1.call-start
  301.7 45.6 %gates0.1 = (bf16[2048,3200]{1,0:T(8,128)(2,1)}, bf16[2048,3200]{1,0:T(8,128)(2,1)}) custom-call(bf16[2048,1024]{1,0:T(8,128)(2,1)} %states1.1.by_ref.b_ref, bf16[2,3200,1024]{2,1,0:T(8,128)(2,1)} %get-tuple-element.22.w_ref, f32[2,2048,3200]{2,1,0:T(8,128)} %get-tuple-element.23.g_ref, f32[2,2048,3200]{2,1,0:T(8,128)} %get-tuple-element.24.u_ref), custom_call_target="tpu_custom_call" | custom-call | flops 13421772800 | bytes 20971520 | tf_op jit(solution)/shard_map/gates0/pallas_call | solution.py:449
  347.2 21.6 %dw_up0.1 = bf16[1024,3200]{1,0:T(8,128)(2,1)} custom-call(bf16[2,2048,1024]{2,1,0:T(8,128)(2,1)} %get-tuple-element.21.a_ref, bf16[2048,3200]{1,0:T(8,128)(2,1)} %get-tuple-element.31.b_ref), custom_call_target="tpu_custom_call" | custom-call | flops 13421772800 | bytes 20971520 | tf_op jit(solution)/shard_map/dw_up0/pallas_call | solution.py:426
  368.8 0.1 reduce-scatter.11.cloned.1.call-update
  368.9 0.1 reduce-scatter.13.cloned.1.call-start
  369.0 21.8 %dw_up1.1 = bf16[1024,3200]{1,0:T(8,128)(2,1)} custom-call(bf16[2,2048,1024]{2,1,0:T(8,128)(2,1)} %get-tuple-element.21.a_ref, bf16[2048,3200]{1,0:T(8,128)(2,1)} %get-tuple-element.26.du_ref.b_ref), custom_call_target="tpu_custom_call" | custom-call | flops 13421772800 | bytes 20971520 | tf_op jit(solution)/shard_map/dw_up1/pallas_call | solution.py:426
  390.8 0.1 reduce-scatter.13.cloned.1.call-update
  390.8 0.1 reduce-scatter.7.cloned.1.call-start
  390.9 21.7 %dw_gate0.1 = bf16[1024,3200]{1,0:T(8,128)(2,1)} custom-call(bf16[2,2048,1024]{2,1,0:T(8,128)(2,1)} %get-tuple-element.21.a_ref, bf16[2048,3200]{1,0:T(8,128)(2,1)} %get-tuple-element.30.b_ref), custom_call_target="tpu_custom_call" | custom-call | flops 13421772800 | bytes 20971520 | tf_op jit(solution)/shard_map/dw_gate0/pallas_call | solution.py:426
  412.6 0.1 reduce-scatter.7.cloned.1.call-update
  412.6 0.1 reduce-scatter.9.cloned.1.call-start
  412.7 21.7 %dw_gate1.1 = bf16[1024,3200]{1,0:T(8,128)(2,1)} custom-call(bf16[2,2048,1024]{2,1,0:T(8,128)(2,1)} %get-tuple-element.21.a_ref, bf16[2048,3200]{1,0:T(8,128)(2,1)} %get-tuple-element.25.dg_ref.b_ref), custom_call_target="tpu_custom_call" | custom-call | flops 13421772800 | bytes 20971520 | tf_op jit(solution)/shard_map/dw_gate1/pallas_call | solution.py:426
  434.4 0.0 copy-start
  434.4 0.1 reduce-scatter.9.cloned.1.call-update
  434.4 0.0 reduce-scatter.15.cloned.1.call-done
  434.5 0.0 reduce-scatter.17.cloned.1.call-done
  434.5 1.8 copy-done
  436.3 6.1 %fusion.10 = (bf16[2,400,1024]{2,1,0:T(8,128)(2,1)}, f32[2,400,1024]{2,1,0:T(8,128)}, f32[2,400,1024]{2,1,0:T(8,128)}) fusion(bf16[2,400,1024]{2,1,0:T(8,128)(2,1)} %wd_ref.1, bf16[1,400,1024]{2,1,0:T(8,128)(2,1)} %bitcast.12, bf16[1,400,1024]{2,1,0:T(8,128)(2,1)} %bitcast.11, f32[2,400,1024]{2,1,0:T(8,128)S(1)} %copy-done, f32[2,400,1024]{2,1,0:T(8,128)} %param.18), kind=kLoop, calls=%fused_computation.22 | loop fusion | flops 15564800 | bytes 18022400 | tf_op jit(solution)/shard_map/convert_element_type | solution.py:482
  442.4 0.0 reduce-scatter.11.cloned.1.call-done
  442.4 7.6 %reduce-scatter.13.cloned.1.call-done = bf16[128,3200]{1,0:T(8,128)(2,1)} async-done(((bf16[1024,3200]{1,0:T(8,128)(2,1)}), bf16[128,3200]{1,0:T(8,128)(2,1)}) %reduce-scatter.13.cloned.1.call-update) | async-done | bytes 819216 | tf_op jit(solution)/shard_map/reduce_scatter | solution.py:490
  450.0 0.0 copy-start.1
  450.0 6.8 %fusion.6 = (bf16[2,128,3200]{2,1,0:T(8,128)(2,1)}, f32[2,128,3200]{2,1,0:T(8,128)}, f32[2,128,3200]{2,1,0:T(8,128)}) fusion(bf16[2,128,3200]{2,1,0:T(8,128)(2,1)} %wu_ref.1, bf16[1,128,3200]{2,1,0:T(8,128)(2,1)} %bitcast.14, bf16[1,128,3200]{2,1,0:T(8,128)(2,1)} %bitcast.13, f32[2,128,3200]{2,1,0:T(8,128)} %param.20, f32[2,128,3200]{2,1,0:T(8,128)} %param.17), kind=kLoop, calls=%fused_computation.18 | loop fusion | flops 15564800 | bytes 18022400 | tf_op jit(solution)/shard_map/convert_element_type | solution.py:482
  456.8 34.7 %reduce-scatter.7.cloned.1.call-done = bf16[128,3200]{1,0:T(8,128)(2,1)} async-done(((bf16[1024,3200]{1,0:T(8,128)(2,1)}), bf16[128,3200]{1,0:T(8,128)(2,1)}) %reduce-scatter.7.cloned.1.call-update) | async-done | bytes 819216 | tf_op jit(solution)/shard_map/reduce_scatter | solution.py:490
  491.6 41.5 %reduce-scatter.9.cloned.1.call-done = bf16[128,3200]{1,0:T(8,128)(2,1)} async-done(((bf16[1024,3200]{1,0:T(8,128)(2,1)}), bf16[128,3200]{1,0:T(8,128)(2,1)}) %reduce-scatter.9.cloned.1.call-update) | async-done | bytes 819216 | tf_op jit(solution)/shard_map/reduce_scatter | solution.py:490
  533.1 0.0 copy-done.1
  533.1 6.1 %fusion.2 = (bf16[2,128,3200]{2,1,0:T(8,128)(2,1)}, f32[2,128,3200]{2,1,0:T(8,128)}, f32[2,128,3200]{2,1,0:T(8,128)}) fusion(bf16[2,128,3200]{2,1,0:T(8,128)(2,1)} %wg_ref.1, bf16[1,128,3200]{2,1,0:T(8,128)(2,1)} %bitcast.16, bf16[1,128,3200]{2,1,0:T(8,128)(2,1)} %bitcast.15, f32[2,128,3200]{2,1,0:T(8,128)S(1)} %copy-done.1, f32[2,128,3200]{2,1,0:T(8,128)} %param.16), kind=kLoop, calls=%fused_computation.14 | loop fusion | flops 15564800 | bytes 18022400 | tf_op jit(solution)/shard_map/convert_element_type | solution.py:482
Async XLA Ops:
  7.2 427.3 %reduce-scatter.15.cloned.1.call-start = ((), (), s32[]{:S(2)}) async-start(), calls=%async_computation.10 | async-start | bytes 7372800 | tf_op jit(solution)/shard_map/reduce_scatter | solution.py:490
  282.8 151.7 %reduce-scatter.17.cloned.1.call-start = ((), (), s32[]{:S(2)}) async-start(), calls=%async_computation.11 | async-start | bytes 7372800 | tf_op jit(solution)/shard_map/reduce_scatter | solution.py:490
  301.6 140.8 %reduce-scatter.11.cloned.1.call-start = ((), (), s32[]{:S(2)}) async-start(), calls=%async_computation.8 | async-start | bytes 7372800 | tf_op jit(solution)/shard_map/reduce_scatter | solution.py:490
  368.9 81.1 %reduce-scatter.13.cloned.1.call-start = ((), (), s32[]{:S(2)}) async-start(), calls=%async_computation.9 | async-start | bytes 7372800 | tf_op jit(solution)/shard_map/reduce_scatter | solution.py:490
  390.8 100.7 %reduce-scatter.7.cloned.1.call-start = ((), (), s32[]{:S(2)}) async-start(), calls=%async_computation.6 | async-start | bytes 7372800 | tf_op jit(solution)/shard_map/reduce_scatter | solution.py:490
  412.6 120.5 %reduce-scatter.9.cloned.1.call-start = ((), (), s32[]{:S(2)}) async-start(), calls=%async_computation.7 | async-start | bytes 7372800 | tf_op jit(solution)/shard_map/reduce_scatter | solution.py:490
  434.4 1.9 copy-start
  450.0 83.1 %copy-start.1 = (f32[2,128,3200]{2,1,0:T(8,128)S(1)}, f32[2,128,3200]{2,1,0:T(8,128)}, u32[]{:S(2)}) copy-start(f32[2,128,3200]{2,1,0:T(8,128)} %param.19) | copy-start | bytes 9830404
Sparse Core Ops, SparseCore 0:
  282.9 39.3 reduce-scatter.14
  324.7 39.3 reduce-scatter.16
  369.0 39.3 reduce-scatter.10
  410.6 39.3 reduce-scatter.12
  452.2 39.3 reduce-scatter.6
  493.7 39.3 reduce-scatter.8
